TPU v7x, 256 devices: a whole 4x4x8 slice. The times are simulated.
256 devices in a mesh: mats: 64 (over z, x, core), tp: 4 (over y).
Axes of the slice: x: 4, y: 4, z: 8, core: 2. Of those that a mesh axis runs over, the one named last changes fastest.
Arguments:
- grad: bfloat16 [3072, 16384], P('tp', 'mats'), may hold values from -40 to 40
- momentum: float32 [3072, 16384], P('tp', 'mats'), may hold values from -6 to 6
Outputs:
- update: bfloat16 [3072, 16384], P('tp', 'mats')
- new_momentum: float32 [3072, 16384], P('tp', 'mats')
All inputs are finite; a program needn't handle non-finite values.
Results may differ from a plain program's by a relative error of at most 0.01.
Values may be sent and summed in bfloat16 or wider, within the bound.
A program may use at most 64 MiB of HBM per device.

v0:
```python
import math
import jax
import jax.numpy as jnp
from jax import lax
from jax.sharding import Mesh
from jax.sharding import PartitionSpec as P

R = 3072
C = 16384
ITERS = 2
MATS = ("mats_0", "mats_1", "mats_2")
momentum_beta = 0.95
first_coef = 3.4445
second_coef = -4.775
third_coef = 2.0315
shape_gain = 0.2
epsilon = 1e-06


def laid_out(tiles, dim):
    tiles = jnp.moveaxis(tiles, 0, dim)
    lengths = tiles.shape
    return tiles.reshape(*lengths[:dim], lengths[dim] * lengths[dim + 1], *lengths[dim + 2 :])


def sent_to_all(array, axis):
    copies = jnp.broadcast_to(array, (lax.axis_size(axis), *array.shape))
    return lax.all_to_all(copies, axis, split_axis=0, concat_axis=0, tiled=True)


def gather_directly(array, axis, dim):
    return laid_out(sent_to_all(array, axis), dim)


def gather_in_order(array, axes, sequence):
    tiles = array[None]
    for k in sequence:
        tiles = lax.all_gather(tiles, axes[k], axis=0, tiled=True)
    block = [lax.axis_size(axes[k]) for k in reversed(sequence)]
    tiles = tiles.reshape(*block, *array.shape)
    turned = sorted(range(len(sequence)), key=lambda place: sequence[len(sequence) - 1 - place])
    return tiles.transpose(*turned, *range(len(sequence), tiles.ndim)).reshape(-1, *array.shape)


def whole_of(array, axes, sequence, dim):
    return laid_out(gather_in_order(array, axes, sequence), dim)


def over_copies(array, axis):
    everything = sent_to_all(array, axis)
    return jnp.sum(everything, axis=0)


def taken_together(array, axis):
    everything = sent_to_all(array, axis)
    return jnp.max(everything, axis=0)


def row_dot(left, right):
    return lax.dot_general(
        left, right, (((1,), (1,)), ((), ())), preferred_element_type=jnp.float32
    )


def per_device(grad, momentum):
    new_momentum = momentum_beta * momentum + grad.astype(jnp.float32)
    iterate = (grad.astype(jnp.float32) + momentum_beta * new_momentum).astype(jnp.bfloat16)
    for step in range(ITERS):
        columns = gather_directly(iterate, "tp", 0)
        partial_gram = row_dot(iterate, columns)
        share = lax.psum_scatter(partial_gram, MATS, scatter_dimension=1, tiled=True).astype(
            jnp.bfloat16
        )
        gram = whole_of(share, MATS, (1, 0, 2), 1)
        if step == 0:
            share_sums = jnp.sum(jnp.abs(share.astype(jnp.float32)), axis=1)
            row_sums = over_copies(share_sums, MATS)
            bound = taken_together(jnp.max(row_sums), "tp") + epsilon
            root = lax.rsqrt(bound)
        first = jnp.dot(gram, columns, preferred_element_type=jnp.float32).astype(jnp.bfloat16)
        second = jnp.dot(
            gram, gather_directly(first, "tp", 0), preferred_element_type=jnp.float32
        ).astype(jnp.bfloat16)
        if step == 0:
            mixed = (
                first_coef * iterate.astype(jnp.float32) * root
                + second_coef * first.astype(jnp.float32) * root**3
                + third_coef * second.astype(jnp.float32) * root**5
            )
        else:
            mixed = (
                first_coef * iterate.astype(jnp.float32)
                + second_coef * first.astype(jnp.float32)
                + third_coef * second.astype(jnp.float32)
            )
        iterate = mixed.astype(jnp.bfloat16)
    update = (shape_gain * math.sqrt(max(R, C)) * iterate.astype(jnp.float32)).astype(jnp.bfloat16)
    return (update, new_momentum)


def solution(mesh):
    split = Mesh(
        mesh.devices.reshape(8, 4, 2, mesh.shape["tp"]), ("mats_0", "mats_1", "mats_2", "tp")
    )
    return jax.shard_map(
        per_device,
        mesh=split,
        in_specs=(P("tp", MATS), P("tp", MATS)),
        out_specs=(P("tp", MATS), P("tp", MATS)),
        check_vma=False,
    )
```

profile of v0, /device:TPU:1, one launch (start us, length us, event | category | flops | bytes accessed | tf_op | source)
XLA Modules:
  0.0 602.9 jit_solution(10310170198701383736)
XLA Ops:
  7.2 0.0 reduce-scatter.3.cloned.1.call-start
  7.2 2.3 fusion.11
  9.5 0.1 broadcast_in_dim.24
  9.6 24.7 %all_to_all.32 = bf16[4,768,256]{2,1,0:T(8,128)(2,1)S(1)} all-to-all(bf16[4,768,256]{2,1,0:T(8,128)(2,1)S(1)} %broadcast_in_dim.24), channel_id=1, replica_groups=mesh['mats_0'=8,'mats_1'=4,'mats_2'=2,'tp'=4] {'tp'}, dimensions={0} | all-to-all | bytes 3145728 | tf_op jit(solution)/shard_map/all_to_all | solution.py:28
  34.3 5.0 fusion.12
  39.3 0.0 reduce-scatter.3.cloned.1.call-update
  39.3 0.0 all-gather.7.cloned.1.call-start
  39.4 153.2 %reduce-scatter.3.cloned.1.call-done = f32[768,48]{0,1:T(8,128)} async-done(((f32[768,3072]{0,1:T(8,128)}), f32[768,48]{0,1:T(8,128)}) %reduce-scatter.3.cloned.1.call-update) | async-done | bytes 147472 | tf_op jit(solution)/shard_map/reduce_scatter | solution.py:71
  192.6 0.9 abs_reduce_fusion
  193.5 9.4 %all-gather = bf16[3072,48]{0,1:T(8,128)(2,1)S(1)} all-gather(bf16[768,48]{0,1:T(8,128)(2,1)S(1)} %get-tuple-element.3), channel_id=2, replica_groups=mesh['mats_0'=8,'mats_1'=4,'mats_2'=2,'tp'=4] {'mats_1'}, dimensions={0}, use_global_device_ids=true | all-gather | bytes 368640 | tf_op jit(solution)/shard_map/all_gather | solution.py:38
  202.9 0.7 copy.30
  203.7 0.0 all-gather.7.cloned.1.call-update
  203.7 0.0 all-gather.9.cloned.1.call-start
  203.8 43.3 %all-gather.7.cloned.1.call-done = bf16[32,768,48]{1,2,0:T(8,128)(2,1)} async-done(((bf16[4,768,48]{1,2,0:T(8,128)(2,1)}), bf16[32,768,48]{1,2,0:T(8,128)(2,1)}) %all-gather.7.cloned.1.call-update) | async-done | bytes 2359312 | tf_op jit(solution)/shard_map/all_gather | solution.py:38
  247.1 0.0 all-gather.9.cloned.1.call-update
  247.1 0.1 broadcast_in_dim.25
  247.2 23.6 %all_to_all.33 = f32[64,1,768]{2,1,0:T(1,128)S(1)} all-to-all(f32[64,1,768]{2,1,0:T(1,128)S(1)} %broadcast_in_dim.25), channel_id=1, replica_groups=mesh['mats_0'=8,'mats_1'=4,'mats_2'=2,'tp'=4] {'mats_0','mats_1','mats_2'}, dimensions={0} | all-to-all | bytes 393216 | tf_op jit(solution)/shard_map/all_to_all | solution.py:28
  270.8 0.1 reduce_sum.19
  270.9 0.6 reduce_max.18
  271.5 1.1 broadcast_in_dim.26
  272.6 4.0 all-to-all-start.2
  276.6 0.0 all-gather.9.cloned.1.call-done
  276.6 2.9 copy.19
  279.5 0.0 copy-start
  279.5 2.1 copy-done
  281.7 1.4 convolution_convert_fusion.3
  283.1 0.0 all-to-all-done.2
  283.1 1.3 broadcast_in_dim.28
  284.4 4.2 all-to-all-start.3
  288.6 0.0 reduce-scatter.5.cloned.1.call-start
  288.6 0.6 reduce_max.19
  289.9 18.3 %all-to-all-done.3 = bf16[4,768,256]{2,1,0:T(8,128)(2,1)S(1)} async-done(((bf16[4,768,256]{2,1,0:T(8,128)(2,1)}), bf16[4,768,256]{2,1,0:T(8,128)(2,1)S(1)}, u32[]{:S(2)}, u32[]{:S(2)}) %all-to-all-start.3) | async-done | bytes 1572896 | tf_op jit(solution)/shard_map/all_to_all | solution.py:28
  308.2 3.8 fusion.9
  312.0 0.1 broadcast_in_dim.29
  312.1 20.9 %all_to_all.34 = bf16[4,768,256]{2,1,0:T(8,128)(2,1)S(1)} all-to-all(bf16[4,768,256]{2,1,0:T(8,128)(2,1)S(1)} %broadcast_in_dim.29), channel_id=1, replica_groups=mesh['mats_0'=8,'mats_1'=4,'mats_2'=2,'tp'=4] {'tp'}, dimensions={0} | all-to-all | bytes 3145728 | tf_op jit(solution)/shard_map/all_to_all | solution.py:28
  332.9 5.0 fusion.13
  338.0 0.0 reduce-scatter.5.cloned.1.call-update
  338.0 0.0 all-gather.11.cloned.1.call-start
  338.1 148.1 %reduce-scatter.5.cloned.1.call-done = f32[768,48]{0,1:T(8,128)} async-done(((f32[768,3072]{0,1:T(8,128)}), f32[768,48]{0,1:T(8,128)}) %reduce-scatter.5.cloned.1.call-update) | async-done | bytes 147472 | tf_op jit(solution)/shard_map/reduce_scatter | solution.py:71
  486.1 0.9 convert_element_type.69
  487.1 9.4 %all-gather.1 = bf16[3072,48]{0,1:T(8,128)(2,1)S(1)} all-gather(bf16[768,48]{0,1:T(8,128)(2,1)S(1)} %convert_element_type.69), channel_id=3, replica_groups=mesh['mats_0'=8,'mats_1'=4,'mats_2'=2,'tp'=4] {'mats_1'}, dimensions={0}, use_global_device_ids=true | all-gather | bytes 368640 | tf_op jit(solution)/shard_map/all_gather | solution.py:38
  496.5 0.7 copy.29
  497.2 0.0 all-gather.11.cloned.1.call-update
  497.3 0.0 all-gather.13.cloned.1.call-start
  497.3 43.7 %all-gather.11.cloned.1.call-done = bf16[32,768,48]{1,2,0:T(8,128)(2,1)} async-done(((bf16[4,768,48]{1,2,0:T(8,128)(2,1)}), bf16[32,768,48]{1,2,0:T(8,128)(2,1)}) %all-gather.11.cloned.1.call-update) | async-done | bytes 2359312 | tf_op jit(solution)/shard_map/all_gather | solution.py:38
  541.0 0.0 all-gather.13.cloned.1.call-update
  541.0 24.6 %all-gather.13.cloned.1.call-done = bf16[64,768,48]{1,2,0:T(8,128)(2,1)} async-done(((bf16[32,768,48]{1,2,0:T(8,128)(2,1)}), bf16[64,768,48]{1,2,0:T(8,128)(2,1)}) %all-gather.13.cloned.1.call-update) | async-done | bytes 4718608 | tf_op jit(solution)/shard_map/all_gather | solution.py:38
  565.6 2.9 copy.21
  568.5 1.4 convolution_convert_fusion.1
  569.9 0.1 broadcast_in_dim.31
  570.0 23.9 %all_to_all.35 = bf16[4,768,256]{2,1,0:T(8,128)(2,1)S(1)} all-to-all(bf16[4,768,256]{2,1,0:T(8,128)(2,1)S(1)} %broadcast_in_dim.31), channel_id=1, replica_groups=mesh['mats_0'=8,'mats_1'=4,'mats_2'=2,'tp'=4] {'tp'}, dimensions={0} | all-to-all | bytes 3145728 | tf_op jit(solution)/shard_map/all_to_all | solution.py:28
  593.9 2.2 fusion.10
Async XLA Ops:
  7.2 185.4 %reduce-scatter.3.cloned.1.call-start = ((), (), s32[]{:S(2)}) async-start(), calls=%async_computation.8 | async-start | bytes 9584640 | tf_op jit(solution)/shard_map/reduce_scatter | solution.py:71
  39.3 207.7 %all-gather.7.cloned.1.call-start = ((), (), s32[]{:S(2)}) async-start(), calls=%async_computation.9 | async-start | bytes 2654208 | tf_op jit(solution)/shard_map/all_gather | solution.py:38
  203.7 72.9 %all-gather.9.cloned.1.call-start = ((), (), s32[]{:S(2)}) async-start(), calls=%async_computation.10 | async-start | bytes 7077888 | tf_op jit(solution)/shard_map/all_gather | solution.py:38
  272.6 10.5 %all-to-all-start.2 = ((f32[4,1,1]{2,1,0:T(1,128)}), f32[4,1,1]{2,1,0:T(1,128)S(1)}, u32[]{:S(2)}, u32[]{:S(2)}) async-start(f32[4,1,1]{2,1,0:T(1,128)} %broadcast_in_dim.26), calls=%async_computation.3 | async-start | bytes 4096 | tf_op jit(solution)/shard_map/all_to_all | solution.py:28
  279.5 2.1 copy-start
  284.4 23.8 %all-to-all-start.3 = ((bf16[4,768,256]{2,1,0:T(8,128)(2,1)}), bf16[4,768,256]{2,1,0:T(8,128)(2,1)S(1)}, u32[]{:S(2)}, u32[]{:S(2)}) async-start(bf16[4,768,256]{2,1,0:T(8,128)(2,1)} %broadcast_in_dim.28), calls=%async_computation.4 | async-start | bytes 3145728 | tf_op jit(solution)/shard_map/all_to_all | solution.py:28
  288.6 197.5 %reduce-scatter.5.cloned.1.call-start = ((), (), s32[]{:S(2)}) async-start(), calls=%async_computation.11 | async-start | bytes 9584640 | tf_op jit(solution)/shard_map/reduce_scatter | solution.py:71
  338.0 203.0 %all-gather.11.cloned.1.call-start = ((), (), s32[]{:S(2)}) async-start(), calls=%async_computation.12 | async-start | bytes 2654208 | tf_op jit(solution)/shard_map/all_gather | solution.py:38
  497.3 68.3 %all-gather.13.cloned.1.call-start = ((), (), s32[]{:S(2)}) async-start(), calls=%async_computation.13 | async-start | bytes 7077888 | tf_op jit(solution)/shard_map/all_gather | solution.py:38
Sparse Core Ops, SparseCore 0:
  39.4 153.0 reduce-scatter.2
  203.8 43.1 all-gather.6
  248.9 22.8 all-gather.8
  338.1 147.9 reduce-scatter.4
  497.4 43.5 all-gather.10
  542.6 22.8 all-gather.12
where the time goes:
time: 603 us
  waiting for transfers between devices  431 us (71%)
  blocking collectives  112 us (19%)
  matrix products  18.9 us (3%)
  between operations  14.9 us (2%)
  local copies, waits for them, and re-layouts  12.2 us (2%)
  starting transfers between devices  8.45 us (1%)
    reduce_scatter x2, waiting for transfers between devices, per_device(): lax.psum_scatter(partial_gram, MATS, scatter_dimension=1, tiled=True)  301 us
    all_gather x4, waiting for transfers between devices, gather_in_order(): tiles = lax.all_gather(tiles, axes[k], axis=0, tiled=True)  112 us
    all_to_all x4, blocking collectives, sent_to_all(): return lax.all_to_all(copies, axis, split_axis=0, concat_axis=0, tiled=True)  93 us
    all_gather x2, blocking collectives, gather_in_order(): tiles = lax.all_gather(tiles, axes[k], axis=0, tiled=True)  18.9 us
    all_to_all x2, waiting for transfers between devices, sent_to_all(): return lax.all_to_all(copies, axis, split_axis=0, concat_axis=0, tiled=True)  18.3 us
  transfers between devices with their start and end apart: 8, of which 6 were waited for; matrix products, arithmetic and copies ran while one was open for 1% of the time, Pallas kernels for 0%

commit v1 on v0

--- a/solution.py
+++ b/solution.py
@@ -35,7 +35,10 @@
 def gather_in_order(array, axes, sequence):
     tiles = array[None]
     for k in sequence:
-        tiles = lax.all_gather(tiles, axes[k], axis=0, tiled=True)
+        devices = lax.axis_size(axes[k])
+        blocks = jnp.stack([tiles for _ in range(devices)])
+        blocks = lax.all_to_all(blocks, axes[k], split_axis=0, concat_axis=0)
+        tiles = jnp.concatenate(blocks, axis=0)
     block = [lax.axis_size(axes[k]) for k in reversed(sequence)]
     tiles = tiles.reshape(*block, *array.shape)
     turned = sorted(range(len(sequence)), key=lambda place: sequence[len(sequence) - 1 - place])

time: 603 us -> 629 us (1.043)
  blocking collectives: 112 us -> 189 us
  waiting for transfers between devices: 431 us -> 375 us
    all_gather x4 -> x0, waiting for transfers between devices: 112 us -> none  [gather_in_order(): tiles = lax.all_gather(tiles, axes[k], axis=0, tiled=True)]
    all_to_all x0 -> x5, blocking collectives: none -> 95 us  [gather_in_order(): blocks = lax.all_to_all(blocks, axes[k], split_axis=0, concat_axis=0)]
    all_to_all x0 -> x1, waiting for transfers between devices: none -> 56.7 us  [gather_in_order(): blocks = lax.all_to_all(blocks, axes[k], split_axis=0, concat_axis=0)]
    all_gather x2 -> x0, blocking collectives: 18.9 us -> none  [gather_in_order(): tiles = lax.all_gather(tiles, axes[k], axis=0, tiled=True)]
  transfers between devices with their start and end apart: 8 -> 5, of which waited for: 6 -> 4; matrix products, arithmetic and copies ran while one was open for 1% -> 1% of each run, Pallas kernels for 0% -> 0%
where the time goes in v1:
time: 629 us
  waiting for transfers between devices  375 us (60%)
  blocking collectives  189 us (30%)
  matrix products  18.9 us (3%)
  between operations  14.9 us (2%)
  starting transfers between devices  12.6 us (2%)
  local copies, waits for them, and re-layouts  10.2 us (2%)
  other arithmetic  8.68 us (1%)
    reduce_scatter x2, waiting for transfers between devices, per_device(): lax.psum_scatter(partial_gram, MATS, scatter_dimension=1, tiled=True)  300 us
    all_to_all x5, blocking collectives, gather_in_order(): blocks = lax.all_to_all(blocks, axes[k], split_axis=0, concat_axis=0)  95 us
    all_to_all x4, blocking collectives, sent_to_all(): return lax.all_to_all(copies, axis, split_axis=0, concat_axis=0, tiled=True)  93.6 us
    all_to_all x1, waiting for transfers between devices, gather_in_order(): blocks = lax.all_to_all(blocks, axes[k], split_axis=0, concat_axis=0)  56.7 us
    all_to_all x2, waiting for transfers between devices, sent_to_all(): return lax.all_to_all(copies, axis, split_axis=0, concat_axis=0, tiled=True)  18.3 us
  transfers between devices with their start and end apart: 5, of which 4 were waited for; matrix products, arithmetic and copies ran while one was open for 1% of the time, Pallas kernels for 0%

profile of v1, /device:TPU:1, one launch (start us, length us, event | category | flops | bytes accessed | tf_op | source)
XLA Modules:
  0.0 628.6 jit_solution(12237874487786093101)
XLA Ops:
  7.2 0.0 reduce-scatter.3.cloned.1.call-start
  7.2 2.3 fusion.11
  9.5 0.1 broadcast_in_dim.18
  9.6 24.7 %all_to_all.62 = bf16[4,768,256]{2,1,0:T(8,128)(2,1)S(1)} all-to-all(bf16[4,768,256]{2,1,0:T(8,128)(2,1)S(1)} %broadcast_in_dim.18), channel_id=1, replica_groups=mesh['mats_0'=8,'mats_1'=4,'mats_2'=2,'tp'=4] {'tp'}, dimensions={0} | all-to-all | bytes 3145728 | tf_op jit(solution)/shard_map/all_to_all | solution.py:28
  34.3 5.0 fusion.12
  39.3 0.0 reduce-scatter.3.cloned.1.call-update
  39.3 153.6 %reduce-scatter.3.cloned.1.call-done = f32[768,48]{0,1:T(8,128)} async-done(((f32[768,3072]{0,1:T(8,128)}), f32[768,48]{0,1:T(8,128)}) %reduce-scatter.3.cloned.1.call-update) | async-done | bytes 147472 | tf_op jit(solution)/shard_map/reduce_scatter | solution.py:74
  192.9 0.9 abs_reduce_fusion
  193.8 8.5 %all_to_all.63 = bf16[4,1,768,48]{2,3,1,0:T(8,128)(2,1)S(1)} all-to-all(bf16[4,1,768,48]{2,3,1,0:T(8,128)(2,1)S(1)} %stack.18), channel_id=1, replica_groups=mesh['mats_0'=8,'mats_1'=4,'mats_2'=2,'tp'=4] {'mats_1'}, dimensions={0} | all-to-all | bytes 589824 | tf_op jit(solution)/shard_map/all_to_all | solution.py:40
  202.4 0.1 broadcast_in_dim.19
  202.5 24.3 %all_to_all.64 = f32[64,1,768]{2,1,0:T(1,128)S(1)} all-to-all(f32[64,1,768]{2,1,0:T(1,128)S(1)} %broadcast_in_dim.19), channel_id=1, replica_groups=mesh['mats_0'=8,'mats_1'=4,'mats_2'=2,'tp'=4] {'mats_0','mats_1','mats_2'}, dimensions={0} | all-to-all | bytes 393216 | tf_op jit(solution)/shard_map/all_to_all | solution.py:28
  226.8 1.6 stack.19
  228.4 4.4 all-to-all-start.4
  232.8 0.2 reduce_sum.19
  233.0 0.6 reduce_max.18
  233.5 56.7 %all-to-all-done.4 = bf16[8,4,768,48]{2,3,1,0:T(8,128)(2,1)} async-done(((bf16[8,4,768,48]{2,3,1,0:T(8,128)(2,1)}), bf16[8,4,768,48]{2,3,1,0:T(8,128)(2,1)}, u32[]{:S(2)}, u32[]{:S(2)}) %all-to-all-start.4) | async-done | bytes 2359328 | tf_op jit(solution)/shard_map/all_to_all | solution.py:40
  290.2 2.8 pad_maximum_fusion
  293.0 8.7 %all_to_all.65 = bf16[2,32,768,48]{2,3,1,0:T(8,128)(2,1)} all-to-all(bf16[2,32,768,48]{2,3,1,0:T(8,128)(2,1)S(1)} %pad_maximum_fusion), channel_id=1, replica_groups=mesh['mats_0'=8,'mats_1'=4,'mats_2'=2,'tp'=4] {'mats_2'}, dimensions={0} | all-to-all | bytes 9437184 | tf_op jit(solution)/shard_map/all_to_all | solution.py:40
  301.7 1.1 broadcast_in_dim.20
  302.8 4.0 all-to-all-start.2
  306.8 2.9 copy.12
  309.7 0.0 copy-start
  309.7 2.1 copy-done
  311.8 1.4 convolution_convert_fusion.3
  313.2 0.0 all-to-all-done.2
  313.2 1.3 broadcast_in_dim.21
  314.5 4.2 all-to-all-start.6
  318.8 0.0 reduce-scatter.5.cloned.1.call-start
  318.8 0.6 reduce_max.19
  320.1 18.3 %all-to-all-done.6 = bf16[4,768,256]{2,1,0:T(8,128)(2,1)S(1)} async-done(((bf16[4,768,256]{2,1,0:T(8,128)(2,1)}), bf16[4,768,256]{2,1,0:T(8,128)(2,1)S(1)}, u32[]{:S(2)}, u32[]{:S(2)}) %all-to-all-start.6) | async-done | bytes 1572896 | tf_op jit(solution)/shard_map/all_to_all | solution.py:28
  338.4 3.8 fusion.9
  342.1 0.1 broadcast_in_dim.22
  342.2 20.9 %all_to_all.66 = bf16[4,768,256]{2,1,0:T(8,128)(2,1)S(1)} all-to-all(bf16[4,768,256]{2,1,0:T(8,128)(2,1)S(1)} %broadcast_in_dim.22), channel_id=1, replica_groups=mesh['mats_0'=8,'mats_1'=4,'mats_2'=2,'tp'=4] {'tp'}, dimensions={0} | all-to-all | bytes 3145728 | tf_op jit(solution)/shard_map/all_to_all | solution.py:28
  363.1 5.0 fusion.13
  368.2 0.0 reduce-scatter.5.cloned.1.call-update
  368.2 146.2 %reduce-scatter.5.cloned.1.call-done = f32[768,48]{0,1:T(8,128)} async-done(((f32[768,3072]{0,1:T(8,128)}), f32[768,48]{0,1:T(8,128)}) %reduce-scatter.5.cloned.1.call-update) | async-done | bytes 147472 | tf_op jit(solution)/shard_map/reduce_scatter | solution.py:74
  514.4 0.9 convert_element_type.69
  515.4 9.0 %all_to_all.67 = bf16[4,1,768,48]{2,3,1,0:T(8,128)(2,1)S(1)} all-to-all(bf16[4,1,768,48]{2,3,1,0:T(8,128)(2,1)S(1)} %stack.21), channel_id=1, replica_groups=mesh['mats_0'=8,'mats_1'=4,'mats_2'=2,'tp'=4] {'mats_1'}, dimensions={0} | all-to-all | bytes 589824 | tf_op jit(solution)/shard_map/all_to_all | solution.py:40
  524.3 0.2 stack.22
  524.5 52.7 %all_to_all.68 = bf16[8,4,768,48]{2,3,1,0:T(8,128)(2,1)S(1)} all-to-all(bf16[8,4,768,48]{2,3,1,0:T(8,128)(2,1)S(1)} %stack.22), channel_id=1, replica_groups=mesh['mats_0'=8,'mats_1'=4,'mats_2'=2,'tp'=4] {'mats_0'}, dimensions={0} | all-to-all | bytes 4718592 | tf_op jit(solution)/shard_map/all_to_all | solution.py:40
  577.2 0.4 pad_maximum_fusion.1
  577.6 16.1 %all_to_all.69 = bf16[2,32,768,48]{2,3,1,0:T(8,128)(2,1)S(1)} all-to-all(bf16[2,32,768,48]{2,3,1,0:T(8,128)(2,1)S(1)} %pad_maximum_fusion.1), channel_id=1, replica_groups=mesh['mats_0'=8,'mats_1'=4,'mats_2'=2,'tp'=4] {'mats_2'}, dimensions={0} | all-to-all | bytes 9437184 | tf_op jit(solution)/shard_map/all_to_all | solution.py:40
  593.7 0.6 copy.13
  594.3 1.4 convolution_convert_fusion.1
  595.8 0.1 broadcast_in_dim.23
  595.9 23.7 %all_to_all.70 = bf16[4,768,256]{2,1,0:T(8,128)(2,1)S(1)} all-to-all(bf16[4,768,256]{2,1,0:T(8,128)(2,1)S(1)} %broadcast_in_dim.23), channel_id=1, replica_groups=mesh['mats_0'=8,'mats_1'=4,'mats_2'=2,'tp'=4] {'tp'}, dimensions={0} | all-to-all | bytes 3145728 | tf_op jit(solution)/shard_map/all_to_all | solution.py:28
  619.6 2.2 fusion.10
  (2 shorter events, 0.0 us)
Async XLA Ops:
  7.2 185.7 %reduce-scatter.3.cloned.1.call-start = ((), (), s32[]{:S(2)}) async-start(), calls=%async_computation.14 | async-start | bytes 9584640 | tf_op jit(solution)/shard_map/reduce_scatter | solution.py:74
  228.4 61.8 %all-to-all-start.4 = ((bf16[8,4,768,48]{2,3,1,0:T(8,128)(2,1)}), bf16[8,4,768,48]{2,3,1,0:T(8,128)(2,1)}, u32[]{:S(2)}, u32[]{:S(2)}) async-start(bf16[8,4,768,48]{2,3,1,0:T(8,128)(2,1)} %stack.19), calls=%async_computation.5 | async-start | bytes 4718592 | tf_op jit(solution)/shard_map/all_to_all | solution.py:40
  302.8 10.4 %all-to-all-start.2 = ((f32[4,1,1]{2,1,0:T(1,128)}), f32[4,1,1]{2,1,0:T(1,128)S(1)}, u32[]{:S(2)}, u32[]{:S(2)}) async-start(f32[4,1,1]{2,1,0:T(1,128)} %broadcast_in_dim.20), calls=%async_computation.3 | async-start | bytes 4096 | tf_op jit(solution)/shard_map/all_to_all | solution.py:28
  309.7 2.1 copy-start
  314.5 23.8 %all-to-all-start.6 = ((bf16[4,768,256]{2,1,0:T(8,128)(2,1)}), bf16[4,768,256]{2,1,0:T(8,128)(2,1)S(1)}, u32[]{:S(2)}, u32[]{:S(2)}) async-start(bf16[4,768,256]{2,1,0:T(8,128)(2,1)} %broadcast_in_dim.21), calls=%async_computation.7 | async-start | bytes 3145728 | tf_op jit(solution)/shard_map/all_to_all | solution.py:28
  318.8 195.6 %reduce-scatter.5.cloned.1.call-start = ((), (), s32[]{:S(2)}) async-start(), calls=%async_computation.15 | async-start | bytes 9584640 | tf_op jit(solution)/shard_map/reduce_scatter | solution.py:74
Sparse Core Ops, SparseCore 0:
  39.4 153.3 reduce-scatter.2
  368.3 146.0 reduce-scatter.4
